TPU v7x, 32 devices: a whole 2x2x4 slice. The times are simulated.
32 devices in a mesh: tp: 8 (over z, y), fsdp: 4 (over x, core).
Axes of the slice: x: 2, y: 2, z: 4, core: 2. Of those that a mesh axis runs over, the one named last changes fastest.
Arguments:
- hidden: bfloat16 [8192, 1024], P('fsdp')
- labels: int32 [8192], P('fsdp')
- tok_mask: float32 [8192], P('fsdp')
- norm_gain: bfloat16 [1024], replicated
- w_head: bfloat16 [1024, 151936], P('fsdp', 'tp')
Outputs:
- output 1: float32 [], replicated
- output 2: bfloat16 [8192, 1024], P('fsdp')
- output 3: bfloat16 [1024, 151936], P('fsdp', 'tp')
- output 4: float32 [1024], replicated
All inputs are finite; a program needn't handle non-finite values.
Results may differ from a plain program's by a relative error of at most 0.0132744.
Values are sent between devices in bfloat16 or wider.
A program may use at most 1 GiB of HBM per device.

v0:
```python
import functools

import jax
import jax.numpy as jnp
from jax import lax
from jax.experimental import pallas as pl
from jax.experimental.pallas import tpu as pltpu
from jax.sharding import PartitionSpec as P

NORM_EPS = 1e-6
LOG2E = 1.4426950408889634
NEG = -1e30
CHUNK = 512
TOK = 1024
EARLY = (2, 5)
AHEAD = 5
ROUNDS = 2
VMEM_LIMIT = 67_043_328
MESH = pl.DeviceIdType.MESH
scope = jax.named_scope
f32, bf16 = jnp.float32, jnp.bfloat16


def dot_nt(a, b):
    return lax.dot_general(a, b, (((1,), (1,)), ((), ())), preferred_element_type=f32)


def dot_tn(a, b):
    return lax.dot_general(a, b, (((0,), (0,)), ((), ())), preferred_element_type=f32)


def dot_nn(a, b):
    return lax.dot_general(a, b, (((1,), (0,)), ((), ())), preferred_element_type=f32)


def cols(k, size):
    return pl.ds(pl.multiple_of(k * size, size), size)


def rows_at(row0, rows):
    return pl.ds(pl.multiple_of(row0, 16), rows)


class Sizes:
    def __init__(self, vocab_tp, n_fsdp, chunk):
        self.n = n_fsdp
        self.rows = -(-vocab_tp // (n_fsdp * 16)) * 16
        self.short = n_fsdp * self.rows - vocab_tp
        self.full = self.rows // chunk
        self.rem = self.rows - self.full * chunk
        self.solid = self.rem - self.short
        assert self.rem > self.short and self.rem % 16 == 0 and self.short % 16 == 0


class Place:
    def __init__(self, n_fsdp, n_tp):
        self.n_fsdp, self.n_tp, self.n_all = n_fsdp, n_tp, n_fsdp * n_tp
        self.f, self.tp = lax.axis_index('fsdp'), lax.axis_index('tp')
        self.x, self.c = self.f // 2, lax.rem(self.f, 2)
        self.n_z = n_tp // 2
        self.z, self.y = self.tp // 2, lax.rem(self.tp, 2)
        self.index = self.tp * n_fsdp + self.f

    def other(self, k):
        i = lax.rem(self.index + k, self.n_all)
        return i // self.n_fsdp, lax.rem(i, self.n_fsdp)

    def every(self, fn):
        def go(k, _):
            fn(k)
            return 0
        lax.fori_loop(1, self.n_all, go, 0)


def dev(tp, f):
    return {'tp': tp, 'fsdp': f}


def rcopy(src, dst, ssem, rsem, to):
    return pltpu.make_async_remote_copy(src_ref=src, dst_ref=dst, send_sem=ssem, recv_sem=rsem, device_id=to, device_id_type=MESH)


def enter(at):
    barrier = pltpu.get_barrier_semaphore()

    def tell(k):
        tp, f = at.other(k)
        pl.semaphore_signal(barrier, inc=1, device_id=dev(tp, f), device_id_type=MESH)

    at.every(tell)
    pl.semaphore_wait(barrier, at.n_all - 1)


def head_kernel(sz, n_tp, vocab_tp, chunk, tok, early,
                h_hbm, lab_ref, mask_ref, gain, w_hbm,
                dw_hbm, gh_hbm, gg_out, l_hbm, g_hbm, h_all, ds_hbm,
                z, w, l0, l1, l2, l3, g0, g1, g2, g3, q0, q1, m, s, scale, lab, lab_in, mask_in, st_loc, got, res, st, top_row, hit, hid,
                acc, stage, sib_out, sib_in, y_sum, y_out, y_in, part, z_out, z_in, z_own, x_out, x_in, gh, gg, gg_in,
                w_s, w_r, loc, hsem, lsem, gsem, qsem, bsem, vsem, ssend, srecv, rsend, rrecv, tok_s, tok_r, blk, hx_s, hx_r, hz_s, hz_r, hy_s, hy_r, hc_s, hc_r,
                hid_sem, dw_copy, dw_send, dw_recv, own_sem, sib_s, sib_r, y_s, y_r, zz_s, zz_r, x_s, x_r, ag_s, ag_r, fw_s, fw_r, gh_sem, gain_s, gain_r):
    at = Place(sz.n, n_tp)
    me, n, n_z, width = at.f, sz.n, at.n_z, w_hbm.shape[1]
    per_f, d = h_hbm.shape
    tokens, own = per_f * n, per_f // n_tp
    lbufs, gbufs, qbufs = (l0, l1, l2, l3), (g0, g1, g2, g3), (q0, q1)
    far, sib = 1 - at.x, at.x * 2 + 1 - at.c
    through = far * 2 + at.c
    sibling, y_peer, x_peer = dev(at.tp, sib), dev(at.z * 2 + 1 - at.y, me), dev(at.tp, through)
    row_rem = sz.full * chunk
    row_odd = row_rem + sz.solid

    with scope('enter'):
        enter(at)

    def slab(f, tp):
        return pl.ds(pl.multiple_of((f * n_tp + tp) * own, own), own)

    def block(f):
        return pl.ds(pl.multiple_of(f * per_f, per_f), per_f)

    own2 = own // 2

    def part_of(f, tp, p):
        return pl.ds(pl.multiple_of((f * n_tp + tp) * own + p * own2, own2), own2)

    def h_to_x(p):
        return rcopy(h_hbm.at[pl.ds(pl.multiple_of(at.tp * own + p * own2, own2), own2), :], h_all.at[part_of(me, at.tp, p), :], hx_s.at[p], hx_r.at[p], x_peer)

    def h_from_x(p):
        here = h_all.at[part_of(through, at.tp, p), :]
        return rcopy(here, here, hx_s.at[p], hx_r.at[p], x_peer)

    def block_out():
        return rcopy(h_hbm, h_all.at[block(me), :], blk.at[0], blk.at[1], sibling)

    def block_in():
        return rcopy(h_hbm, h_all.at[block(sib), :], blk.at[0], blk.at[1], sibling)

    def moved(tp, ssem, rsem, to):
        here = h_all.at[slab(through, tp), :]
        return rcopy(here, here, ssem, rsem, to)

    def z_from(jj):
        return lax.rem(at.z + n_z - jj - 1, n_z)

    def h_to_z(jj, p):
        here = h_all.at[part_of(through, at.tp, p), :]
        return rcopy(here, here, hz_s.at[jj, p], hz_r.at[jj, p], dev(lax.rem(at.z + jj + 1, n_z) * 2 + at.y, me))

    def h_from_z(jj, p):
        here = h_all.at[part_of(through, z_from(jj) * 2 + at.y, p), :]
        return rcopy(here, here, hz_s.at[jj, p], hz_r.at[jj, p], sibling)

    def h_to_y(zo):
        return moved(zo * 2 + at.y, hy_s.at[zo], hy_r.at[zo], y_peer)

    def h_from_y(zo):
        return moved(zo * 2 + 1 - at.y, hy_s.at[zo], hy_r.at[zo], y_peer)

    def h_to_core(tp):
        return moved(tp, hc_s.at[tp], hc_r.at[tp], sibling)

    def h_from_core(tp):
        here = h_all.at[slab(far * 2 + 1 - at.c, tp), :]
        return rcopy(here, here, hc_s.at[tp], hc_r.at[tp], sibling)

    def tok_out(k):
        to = dev(at.tp, lax.rem(me + k, n))
        return [rcopy(lab_ref, lab_in.at[me], tok_s.at[0, k], tok_r.at[0, k], to), rcopy(mask_ref, mask_in.at[me], tok_s.at[1, k], tok_r.at[1, k], to)]

    def tok_in(k):
        src = lax.rem(me + n - k, n)
        return [rcopy(lab_ref, lab_in.at[src], tok_s.at[0, k], tok_r.at[0, k], sibling), rcopy(mask_ref, mask_in.at[src], tok_s.at[1, k], tok_r.at[1, k], sibling)]

    for p in (0, 1):
        h_to_x(p).start()
    block_out().start()
    for k in range(1, n):
        for cp in tok_out(k):
            cp.start()
    lab_in[me] = lab_ref[...]
    mask_in[me] = mask_ref[...]

    def remote(k, c, row0, rows):
        dest = lax.rem(me + k, n)
        return rcopy(w_hbm.at[rows_at(dest * sz.rows + row0, rows), :], w.at[rows_at(row0, rows), cols(me, width)], w_s.at[c, k], w_r.at[c, k], dev(at.tp, dest))

    def arrival(k, c, row0, rows):
        src = lax.rem(me + n - k, n)
        return rcopy(w_hbm.at[pl.ds(0, rows), :], w.at[rows_at(row0, rows), cols(src, width)], w_s.at[c, k], w_r.at[c, k], sibling)

    def local(c, row0, rows):
        return pltpu.make_async_copy(w_hbm.at[rows_at(me * sz.rows + row0, rows), :], w.at[rows_at(row0, rows), cols(me, width)], loc.at[c])

    def issue(c):
        local(c, c * chunk, chunk).start()
        for k in range(1, n):
            remote(k, c, c * chunk, chunk).start()

    def when_not_last(dest, fn):
        if sz.short:
            pl.when(dest != n - 1)(fn)

    def issue_rem():
        local(sz.full, row_rem, sz.solid).start()
        when_not_last(me, lambda: local(sz.full + 1, row_odd, sz.short).start())
        for k in range(1, n):
            remote(k, sz.full, row_rem, sz.solid).start()
            when_not_last(lax.rem(me + k, n), lambda: remote(k, sz.full + 1, row_odd, sz.short).start())

    ahead = min(AHEAD, sz.full)
    for c in range(ahead):
        issue(c)
    if sz.short:
        @pl.when(me == n - 1)
        def _():
            w[row_odd:, :] = jnp.zeros((sz.short, d), bf16)

    sub = min(256, own)
    slices, per_own = per_f // sub, own // sub
    lane = min(128, sub)

    def place(t, i):
        near = jnp.where(t == 0, me, sib) * per_f + i * sub
        j = i // per_own
        f = jnp.where(j < n_z, through, far * 2 + 1 - at.c)
        y = jnp.where(t == 2, at.y, 1 - at.y)
        away = (f * n_tp + lax.rem(j, n_z) * 2 + y) * own + lax.rem(i, per_own) * sub
        return pl.multiple_of(jnp.where(t < 2, near, away), sub)

    def norm(t):
        def load(i):
            here = pl.ds(place(t, i), sub)
            return pltpu.make_async_copy(h_hbm.at[cols(i, sub), :] if t == 0 else h_all.at[here, :], z.at[here, :], hsem.at[i])

        def begin(i, _):
            load(i).start()
            return 0

        def one(i, _):
            load(i).wait()
            here = pl.ds(place(t, i), sub)
            h = z[here, :].astype(f32)
            inv = lax.rsqrt(jnp.mean(h * h, axis=-1, keepdims=True) + NORM_EPS)
            z[here, :] = (h * inv * gain[...].astype(f32)[None, :]).astype(bf16)
            return 0

        with scope(f'norm{t}'):
            lax.fori_loop(0, slices, begin, 0)
            lax.fori_loop(0, slices, one, 0)

    def spread_x(p):
        with scope('x_wait'):
            h_from_x(p).wait_recv()
        for jj in (2, 0, 1):
            if jj < n_z - 1:
                h_to_z(jj, p).start()

    norm(0)
    spread_x(0)
    with scope('blk_wait'):
        block_in().wait_recv()
    norm(1)
    spread_x(1)
    h_to_y(at.z).start()
    h_to_core(at.tp).start()
    with scope('tok_wait'):
        for k in range(1, n):
            for cp in tok_in(k):
                cp.wait_recv()
    count = jnp.sum(mask_in[...], axis=(0, 2), keepdims=True)[0]
    for f in range(n):
        here = pl.ds(f * per_f, per_f)
        scale[0:1, here] = mask_in[f] / count
        rel = lab_in[f] - at.tp * vocab_tp
        lab[0:1, here] = jnp.where(jnp.logical_and(rel >= 0, rel < vocab_tp), rel - me * sz.rows, -1)

    def spread_z():
        with scope('z_wait'):
            for jj in range(n_z - 1):
                for p in (0, 1):
                    h_from_z(jj, p).wait_recv()
                h_to_y(z_from(jj)).start()
                h_to_core(z_from(jj) * 2 + at.y).start()

    def spread_y():
        with scope('hy_wait'):
            for k in range(n_z):
                zo = lax.rem(at.z + n_z - k, n_z)
                h_from_y(zo).wait_recv()
                h_to_core(zo * 2 + 1 - at.y).start()

    def far_ready(y):
        with scope('core_wait'):
            for zo in range(n_z):
                h_from_core(zo * 2 + y).wait_recv()

    m[...] = jnp.full(m.shape, NEG, f32)
    s[...] = jnp.zeros(s.shape, f32)
    per_buf = tok // sub
    n_buf = slices // per_buf

    def out_copies(row0, rows, t, b):
        return [pltpu.make_async_copy(lbufs[b * n_buf + i // per_buf].at[pl.ds(0, rows), pl.ds(i % per_buf * sub, sub)],
                                      l_hbm.at[rows_at(row0, rows), pl.ds(place(t, i), sub)], lsem.at[b * n_buf + i // per_buf]) for i in range(slices)]

    def out_done(rows, b):
        for i in range(n_buf):
            pltpu.make_async_copy(lbufs[b * n_buf + i].at[pl.ds(0, rows), :], l_hbm.at[pl.ds(0, rows), pl.ds(0, tok)], lsem.at[b * n_buf + i]).wait()

    def statistics(read, rows, t0):
        group = min(4, rows // 8)
        for c1 in range(0, sub, lane):
            sl = pl.ds(pl.multiple_of(t0 + c1, lane), lane)
            big, tot = m[:, sl], s[:, sl]
            for g in range(0, rows // 8, group):
                piece = [read(r, c1) for r in range(g, min(g + group, rows // 8))]
                new = functools.reduce(jnp.maximum, piece, big)
                tot = tot * jnp.exp2(big - new)
                for x in piece:
                    tot += jnp.exp2(x - new)
                big = new
            m[:, sl], s[:, sl] = big, tot

    def slice_at(b, i):
        return lbufs[b * n_buf + i // per_buf], i % per_buf * sub

    def late_statistics(t, b):
        for i in range(slices - lag, slices):
            buf, i0 = slice_at(b, i)
            statistics(lambda r, c1: buf[8 * r:8 * r + 8, i0 + c1:i0 + c1 + lane], chunk, place(t, i))

    def logits_tile(row0, rows, t, b, masked):
        for i in range(slices):
            t0 = place(t, i)
            logits = dot_nt(w[rows_at(row0, rows), :], z[pl.ds(t0, sub), :]) * LOG2E
            if masked:
                ids = lax.broadcasted_iota(jnp.int32, (rows, sub), 0)
                logits = jnp.where(ids < jnp.where(me == n - 1, sz.solid, sz.rem), logits, NEG)
            buf, i0 = slice_at(b, i)
            buf[0:rows, i0:i0 + sub] = logits
            if masked or i < slices - lag:
                statistics(lambda r, c1: logits[8 * r:8 * r + 8, c1:c1 + lane], rows, t0)

    lag = 2
    for i in range(slices - lag, slices):
        buf, i0 = slice_at(1, i)
        buf[:, i0:i0 + sub] = jnp.full((chunk, sub), NEG, f32)

    n_a = min(3, sz.full)
    n_c = min(3, sz.full - n_a)
    k_b, k_c = 2 * n_a, 3 * n_a
    k_d = k_c + 3 * n_c
    k_e = k_d + n_a + n_c

    def item(k):
        u, v = k - k_c, k - k_e
        c = jnp.where(k < k_b, k // 2, jnp.where(k < k_c, k - k_b, jnp.where(k < k_d, n_a + u // 3, jnp.where(k < k_e, k - k_d, n_a + n_c + v // 4))))
        t = jnp.where(k < k_b, lax.rem(k, 2), jnp.where(k < k_c, 2, jnp.where(k < k_d, lax.rem(u, 3), jnp.where(k < k_e, 3, lax.rem(v, 4)))))
        return c, t

    def work(i2, _):
        for b in (0, 1):
            k = 2 * i2 + b
            c, t = item(k)

            @pl.when(t == 0)
            def _():
                with scope('w_wait'):
                    local(c, c * chunk, chunk).wait()
                    for j in range(1, n):
                        arrival(j, c, c * chunk, chunk).wait_recv()

                @pl.when(c + ahead < sz.full)
                def _():
                    issue(c + ahead)

                @pl.when(c + ahead == sz.full)
                def _():
                    issue_rem()

            @pl.when(k == k_b)
            def _():
                spread_z()
                far_ready(at.y)
                norm(2)

            @pl.when(k == max(k_d - 3, k_c))
            def _():
                spread_y()

            @pl.when(k == k_d)
            def _():
                far_ready(1 - at.y)
                norm(3)

            with scope('l_wait'):
                @pl.when(k >= 2)
                def _():
                    out_done(chunk, b)
            with scope('l_tile'):
                late_statistics(item(jnp.maximum(k - 1, 0))[1], 1 - b)
                logits_tile(c * chunk, chunk, t, b, False)
            for cp in out_copies(c * chunk, chunk, t, b):
                cp.start()
        return 0

    lax.fori_loop(0, sz.full * 2, work, 0)
    late_statistics(item(4 * sz.full - 1)[1], 1)
    with scope('w_wait_rem'):
        local(sz.full, row_rem, sz.solid).wait()
        when_not_last(me, lambda: local(sz.full + 1, row_odd, sz.short).wait())
        for k in range(1, n):
            arrival(k, sz.full, row_rem, sz.solid).wait_recv()
            when_not_last(me, lambda: arrival(k, sz.full + 1, row_odd, sz.short).wait_recv())

    def work_rem(i2, _):
        for b in (0, 1):
            @pl.when(i2 == 0)
            def _():
                out_done(chunk, b)

            @pl.when(i2 > 0)
            def _():
                out_done(sz.rem, b)
            logits_tile(row_rem, sz.rem, 2 * i2 + b, b, True)
            for cp in out_copies(row_rem, sz.rem, 2 * i2 + b, b):
                cp.start()
        return 0

    with scope('l_rem'):
        lax.fori_loop(0, 2, work_rem, 0)

    big = jnp.max(m[...], axis=0, keepdims=True)
    st_loc[0:1, :] = big
    st_loc[1:2, :] = jnp.sum(s[...] * jnp.exp2(m[...] - big), axis=0, keepdims=True)
    mine = slab(at.f, at.tp)

    def ask(k):
        tp, f = at.other(k)
        return rcopy(st_loc.at[:, slab(f, tp)], got.at[k], ssend.at[k], srecv.at[k], dev(tp, f))

    def answer(k):
        tp, f = at.other(k)
        return rcopy(res, st.at[:, mine], rsend.at[k], rrecv.at[k], dev(tp, f))

    def answered(k):
        tp, f = at.other(at.n_all - k)
        return rcopy(res, st.at[:, slab(f, tp)], rsend.at[k], rrecv.at[k], dev(tp, f))

    n_tok = tokens // tok

    def load_l(row0, rows, k, b):
        return pltpu.make_async_copy(l_hbm.at[rows_at(row0, rows), cols(k, tok)], lbufs[b].at[pl.ds(0, rows), :], lsem.at[b])

    def load_g(row0, rows, k, b):
        return pltpu.make_async_copy(g_hbm.at[rows_at(row0, rows), cols(k, tok)], gbufs[b].at[pl.ds(0, rows), :], gsem.at[b])

    def save_g(row0, rows, k, b):
        return pltpu.make_async_copy(gbufs[b].at[pl.ds(0, rows), :], g_hbm.at[rows_at(row0, rows), cols(k, tok)], gsem.at[b])

    at.every(lambda k: ask(k).start())
    got[0] = st_loc[:, mine]
    for b in (0, 1):
        out_done(sz.rem, b)
    for b in range(4):
        load_l(0, chunk, b, b).start()
    h_load = pltpu.make_async_copy(h_hbm.at[pl.ds(pl.multiple_of(at.tp * own, own), own), :], hid, hid_sem.at[0])
    h_load.start()
    acc[...] = jnp.zeros(acc.shape, f32)
    hit[...] = jnp.zeros(hit.shape, f32)
    with scope('ask_wait'):
        at.every(lambda k: ask(k).wait_recv())
    tops = got[:, 0:1, :]
    top = jnp.max(tops, axis=0)
    res[...] = top + jnp.log2(jnp.sum(got[:, 1:2, :] * jnp.exp2(tops - top[None]), axis=0))
    at.every(lambda k: answer(k).start())
    st[:, mine] = res[...]
    with scope('answer_wait'):
        at.every(lambda k: answered(k).wait_recv())
    top_row[...] = st[...] - jnp.log2(scale[...])

    def gradient(x, sl, row0, count=True):
        rows = x.shape[0]
        sc = scale[0:1, sl]
        x3 = x.reshape(rows // 8, 8, x.shape[1])
        p = jnp.exp2(x3 - top_row[0:1, sl][None])
        is_label = lax.broadcasted_iota(jnp.int32, p.shape, 0) * 8 == (lab[0:1, sl] - row0 - lax.broadcasted_iota(jnp.int32, (8, x.shape[1]), 0))[None]
        if count:
            hit[...] += jnp.sum(jnp.where(is_label, x3, 0.0), axis=0) * sc
        return jnp.where(is_label, p - sc[None], p).reshape(x.shape).astype(bf16)

    step = min(256, tok)

    half = own // ROUNDS

    def grad_tile(row0, rows, k, b, fresh, first_round=0):
        total = None
        for c0 in range(0, tok, step):
            if fresh:
                for c1 in range(c0, c0 + step, lane):
                    gbufs[b][0:rows, c1:c1 + lane] = gradient(lbufs[b][0:rows, c1:c1 + lane], pl.ds(pl.multiple_of(k * tok + c1, lane), lane), row0, c1 % own // half >= first_round)
            p = dot_nn(gbufs[b][0:rows, c0:c0 + step], z[pl.ds(pl.multiple_of(k * tok + c0, step), step), :])
            total = p if total is None else total + p
        acc[0:rows, :] += total

    def aside(c, rows):
        slot = lax.rem(c, 2)
        return pltpu.make_async_copy(stage.at[slot, pl.ds(0, rows), :], ds_hbm.at[rows_at(c * chunk, rows), :], dw_copy.at[slot])

    def keep_own(c, rows):
        slot = lax.rem(c, 2)
        return pltpu.make_async_copy(stage.at[slot, pl.ds(0, rows), cols(me, width)], dw_hbm.at[rows_at(me * sz.rows + c * chunk, rows), :], own_sem.at[slot])

    def sends(c, rows):
        out = []
        for i, f in enumerate((far * 2, far * 2 + 1, sib)):
            out.append(rcopy(ds_hbm.at[rows_at(c * chunk, rows), cols(f, width)], dw_hbm.at[rows_at(me * sz.rows + c * chunk, rows), :],
                             dw_send.at[c, i], dw_recv.at[lax.rem(f + n - me, n)], dev(at.tp, f)))
        return out

    def ship(c, rows):
        with scope('ship'):
            stage[lax.rem(c, 2), 0:rows, :] = acc[0:rows, :].astype(bf16)
            acc[...] = jnp.zeros(acc.shape, f32)
        aside(c, rows).start()
        keep_own(c, rows).start()

    def flush(c, rows):
        aside(c, rows).wait()
        keep_own(c, rows).wait()
        for cp in sends(c, rows):
            cp.start()

    def early_chunks(lo, hi, first_round, after):
        def one(c, _):
            def quad(i, _):
                for b in range(4):
                    k = 4 * i + b
                    with scope('b1_wait'):
                        load_l(0, chunk, 0, b).wait()

                        @pl.when(jnp.logical_not(jnp.logical_and(c == lo, i == 0)))
                        def _():
                            save_g(0, chunk, 0, b).wait()
                    with scope('b1_tile'):
                        grad_tile(c * chunk, chunk, k, b, True, first_round)
                    save_g(c * chunk, chunk, k, b).start()
                    wrap = k + 4 >= n_tok
                    c2 = jnp.where(wrap, c + 1, c)

                    @pl.when(c2 < hi)
                    def _():
                        load_l(c2 * chunk, chunk, jnp.where(wrap, k + 4 - n_tok, k + 4), b).start()

                @pl.when(jnp.logical_and(i == 0, c > lo))
                def _():
                    flush(c - 1, chunk)
                return 0
            lax.fori_loop(0, n_tok // 4, quad, 0)
            ship(c, chunk)
            after(c)
            return 0
        lax.fori_loop(lo, hi, one, 0)
        for b in range(4):
            save_g(0, chunk, 0, b).wait()

    early_chunks(0, early[0], 0, lambda c: None)

    groups = 2 * n_z
    last = ROUNDS * groups

    def low(e):
        return [(j, chunk) for j in range(sz.full - e)] + [(sz.full - e, sz.rem)]
    per_l = tok // half

    def group_of(q):
        r, g = q // groups, lax.rem(q, groups)
        xi, jj = g // n_z, lax.rem(g, n_z)
        return r, xi, jj, jnp.where(xi == 0, far, at.x), lax.rem(at.z + jj + 1, n_z)

    def pieces(q, b):
        r, _, _, xb, zb = group_of(q)
        cb = at.c if b == 1 else 1 - at.c
        return [pl.multiple_of((xb * 2 + cb) * per_f + (zb * 2 + yb) * own + r * half, half) for yb in (1 - at.y, at.y)]

    def l_part(b, j, i, rows):
        p = 2 * j + i
        return lbufs[2 * b + p // per_l].at[pl.ds(0, rows), pl.ds(p % per_l * half, half)]

    def block_loads(q, b, e):
        row_low = e * chunk
        out = []
        for i, t0 in enumerate(pieces(q, b)):
            out.append(pltpu.make_async_copy(g_hbm.at[pl.ds(0, row_low), pl.ds(t0, half)], qbufs[b].at[pl.ds(0, row_low), pl.ds(i * half, half)], qsem.at[b, i]))
            for j, rows in low(e):
                out.append(pltpu.make_async_copy(l_hbm.at[pl.ds(row_low + j * chunk, rows), pl.ds(t0, half)], l_part(b, j, i, rows), bsem.at[b, 2 * j + i]))
        return out

    def block_saves(q, b, e):
        row_low = e * chunk
        return [pltpu.make_async_copy(qbufs[b].at[pl.ds(row_low, sz.rows - row_low), pl.ds(i * half, half)],
                                      g_hbm.at[pl.ds(row_low, sz.rows - row_low), pl.ds(t0, half)], vsem.at[b, i]) for i, t0 in enumerate(pieces(q, b))]

    def block_dot(q, b, e):
        row_low = e * chunk
        for i, t0 in enumerate(pieces(q, b)):
            for j, rows in low(e):
                row0 = row_low + j * chunk
                qbufs[b][row0:row0 + rows, i * half:(i + 1) * half] = gradient(l_part(b, j, i, rows)[...], pl.ds(t0, half), row0)
        return dot_tn(qbufs[b][...], w[...])

    def to_sib(q):
        slot = lax.rem(q, 2)
        return rcopy(sib_out.at[slot], sib_in.at[slot], sib_s.at[slot], sib_r.at[slot], sibling)

    def to_y(q):
        slot, land = lax.rem(q, 2), lax.rem(q, y_in.shape[0])
        return rcopy(y_out.at[slot], y_in.at[land], y_s.at[slot], y_r.at[land], y_peer)

    def to_z(q):
        r, xi, jj, _, zb = group_of(q)
        return rcopy(z_out.at[jj], z_in.at[r, xi, jj], zz_s.at[jj], zz_r.at[r, xi, jj], dev(zb * 2 + at.y, me))

    def to_x(r):
        return rcopy(x_out, x_in.at[r], x_s.at[0], x_r.at[r], x_peer)

    def z_stage(q):
        _, xi, jj, _, _ = group_of(q)
        with scope('y_wait'):
            to_y(q).wait_recv()
        val = part[lax.rem(q, part.shape[0])] + y_in[lax.rem(q, y_in.shape[0])].astype(f32)

        @pl.when(jj == n_z - 1)
        def _():
            z_own[xi] = val

        @pl.when(jj < n_z - 1)
        def _():
            @pl.when(q >= n_z)
            def _():
                to_z(q - n_z).wait_send()
            z_out[jj] = val.astype(bf16)
            to_z(q).start()

    def z_sum(r, xi):
        val = z_own[xi]
        for jj in range(n_z - 1):
            rcopy(z_out.at[0], z_in.at[r, xi, jj], zz_s.at[jj], zz_r.at[r, xi, jj], sibling).wait_recv()
            val = val + z_in[r, xi, jj].astype(f32)
        return val

    def x_stage(r):
        @pl.when(r > 0)
        def _():
            to_x(0).wait_send()
        with scope('x_stage'):
            x_out[...] = z_sum(r, 0).astype(bf16)
        to_x(r).start()

    def home(tp, r):
        return gh_hbm.at[pl.ds(pl.multiple_of(tp * own + r * half, half), half), :]

    def gathers(r):
        out = [rcopy(gh.at[r], home(at.tp, r), ag_s.at[r, n_z - 1], fw_r.at[r, at.z], y_peer)]
        for jj in (0, 2, 1):
            if jj >= n_z - 1:
                continue
            to = lax.rem(at.z + jj + 1, n_z)
            out.append(rcopy(gh.at[r], home(at.tp, r), ag_s.at[r, jj], ag_r.at[r, jj], dev(to * 2 + at.y, me)))
        return out

    def keep(r):
        return pltpu.make_async_copy(gh.at[r], home(at.tp, r), gh_sem.at[r])

    def arrived(r, jj):
        return rcopy(gh.at[r], home(z_from(jj) * 2 + at.y, r), ag_s.at[r, jj], ag_r.at[r, jj], sibling)

    def onward(r, jj):
        here = home(z_from(jj) * 2 + at.y, r)
        return rcopy(here, here, fw_s.at[r, jj], fw_r.at[r, z_from(jj)], y_peer)

    def tell_gain(k):
        tp, f = at.other(k)
        return rcopy(gg, gg_in.at[at.index], gain_s.at[k], gain_r.at[k], dev(tp, f))

    def heard_gain(k):
        i = lax.rem(at.index + at.n_all - k, at.n_all)
        return rcopy(gg, gg_in.at[i], gain_s.at[k], gain_r.at[k], sibling)

    def final(r):
        with scope('final_wait'):
            to_x(r).wait_recv()
            dz = z_sum(r, 1) + x_in[r].astype(f32)
        h = hid[pl.ds(pl.multiple_of(r * half, half), half), :].astype(f32)
        inv = lax.rsqrt(jnp.mean(h * h, axis=-1, keepdims=True) + NORM_EPS)
        normed = h * inv
        a = dz * gain[...].astype(f32)[None, :]
        gh[r] = (inv * (a - normed * jnp.mean(a * normed, axis=-1, keepdims=True))).astype(bf16)
        gg[0:1, 0:d] += jnp.sum(dz * normed, axis=0, keepdims=True)
        if r == 1:
            hits = jnp.sum(jnp.sum(hit[...], axis=0, keepdims=True), axis=1, keepdims=True)
            gg[0:1, d:] = jnp.broadcast_to(hits, (1, gg.shape[1] - d))
            at.every(lambda k: tell_gain(k).start())
            gg_in[at.index] = gg[...]
        keep(r).start()
        if r == 1:
            gather_start(1)

    def gather_start(r):
        for cp in gathers(r):
            cp.start()

    def forward(r, jj):
        with scope('fw_wait'):
            arrived(r, jj).wait_recv()
        onward(r, jj).start()

    h_load.wait()
    gg[...] = jnp.zeros(gg.shape, f32)

    def dz_round(r, e):
        lo, hi = r * groups, (r + 1) * groups
        for b in (0, 1):
            for cp in block_loads(lo, b, e):
                cp.start()

        def dz_group(q, _):
            for b in (0, 1):
                with scope('a_wait'):
                    for cp in block_loads(q, b, e):
                        cp.wait()

                    @pl.when(q > lo)
                    def _():
                        for cp in block_saves(q - 1, b, e):
                            cp.wait()
                slot = lax.rem(q, 2)
                if b == 0:
                    @pl.when(q >= 2)
                    def _():
                        to_sib(q - 2).wait_send()
                    with scope('a_dot0'):
                        sib_out[slot] = block_dot(q, b, e).astype(bf16)
                    to_sib(q).start()
                else:
                    @pl.when(q >= 2)
                    def _():
                        to_y(q - 2).wait_send()
                    with scope('a_dot1'):
                        val = block_dot(q, b, e)
                        y_sum[...] = val[0:half]
                        part[lax.rem(q, part.shape[0])] = val[half:]
                    with scope('sib_wait'):
                        to_sib(q).wait_recv()
                    y_out[slot] = (y_sum[...] + sib_in[slot, 0:half].astype(f32)).astype(bf16)
                    part[lax.rem(q, part.shape[0])] += sib_in[slot, half:].astype(f32)
                    to_y(q).start()
                for cp in block_saves(q, b, e):
                    cp.start()

                @pl.when(q + 1 < hi)
                def _():
                    for cp in block_loads(q + 1, b, e):
                        cp.start()

            @pl.when(q == lo)
            def _():
                flush(e - 1, chunk)

            @pl.when(q >= lo + 2)
            def _():
                z_stage(q - 2)
            if r == 0:
                @pl.when(q == hi - 1)
                def _():
                    z_stage(q - 1)
            return 0

        lax.fori_loop(lo, hi, dz_group, 0)
        for b in (0, 1):
            for cp in block_saves(hi - 1, b, e):
                cp.wait()

    dz_round(0, early[0])
    for b in range(4):
        load_l(early[0] * chunk, chunk, b, b).start()

    def between(c):
        @pl.when(c == early[0])
        def _():
            z_stage(groups - 1)
            x_stage(0)
            if early[1] - early[0] == 1:
                final(0)
                gather_start(0)

        if early[1] - early[0] > 1:
            @pl.when(c == early[0] + 1)
            def _():
                final(0)
                gather_start(0)

    early_chunks(early[0], early[1], 1, between)
    dz_round(1, early[1])
    z_stage(last - 2)

    for b in range(4):
        load_g(early[1] * chunk, chunk, b, b).start()

    quads = n_tok // 4
    nearest = [jj for jj in (2, 0, 1) if jj < n_z - 1]
    steps = [(t // 2, 0, jj) for t, jj in enumerate(nearest)] + [(6 + t, 1, jj) for t, jj in enumerate(nearest)]

    def late_chunk(c, _):
        def quad(i, _):
            for b in range(4):
                k = 4 * i + b
                with scope('b2_wait'):
                    load_g(0, chunk, 0, b).wait()
                with scope('b2_tile'):
                    grad_tile(c * chunk, chunk, k, b, False)
                wrap = k + 4 >= n_tok
                c2, k2 = jnp.where(wrap, c + 1, c), jnp.where(wrap, k + 4 - n_tok, k + 4)

                @pl.when(c2 < sz.full)
                def _():
                    load_g(c2 * chunk, chunk, k2, b).start()

                @pl.when(c2 == sz.full)
                def _():
                    load_g(row_rem, sz.rem, k2, b).start()
                if b == 0:
                    @pl.when(jnp.logical_and(i == 0, c > early[1]))
                    def _():
                        flush(c - 1, chunk)

            for t, r, jj in steps:
                @pl.when((c - early[1]) * quads + i == t)
                def _():
                    forward(r, jj)
            return 0
        lax.fori_loop(0, quads, quad, 0)
        ship(c, chunk)

        @pl.when(c == early[1])
        def _():
            z_stage(last - 1)
            x_stage(1)

        @pl.when(c == early[1] + 1)
        def _():
            final(1)
        return 0

    lax.fori_loop(early[1], sz.full, late_chunk, 0)
    def late_rem(i, _):
        for b in range(4):
            with scope('b2_wait'):
                load_g(row_rem, sz.rem, 0, b).wait()
            with scope('b2_rem'):
                grad_tile(row_rem, sz.rem, 4 * i + b, b, False)

            @pl.when(4 * i + b + 4 < n_tok)
            def _():
                load_g(row_rem, sz.rem, 4 * i + b + 4, b).start()
            if b == 0:
                @pl.when(i == 0)
                def _():
                    flush(sz.full - 1, chunk)
        return 0

    lax.fori_loop(0, n_tok // 4, late_rem, 0)
    ship(sz.full, sz.rem)
    flush(sz.full, sz.rem)
    for t, r, jj in steps:
        if t >= (sz.full - early[1]) * quads:
            forward(r, jj)

    with scope('t_gain'):
        at.every(lambda k: heard_gain(k).wait_recv())
    total = jnp.sum(gg_in[...], axis=0)
    gg_out[0:1, 0:d] = total[0:1, 0:d]
    gg_out[0:1, d:] = (jnp.sum(st[...] * scale[...], axis=1, keepdims=True) - total[0:1, d:]) * (1.0 / LOG2E)
    with scope('t_small'):
        at.every(lambda k: ask(k).wait_send())
        at.every(lambda k: answer(k).wait_send())
        at.every(lambda k: tell_gain(k).wait_send())
        for k in range(1, n):
            for cp in tok_out(k):
                cp.wait_send()
        block_out().wait_send()
        for p in (0, 1):
            h_to_x(p).wait_send()
            for jj in range(n_z - 1):
                h_to_z(jj, p).wait_send()
        for zo in range(n_z):
            h_to_y(zo).wait_send()
        for tp in range(n_tp):
            h_to_core(tp).wait_send()

        def w_sent(c, _):
            for k in range(1, n):
                remote(k, c, c * chunk, chunk).wait_send()
            return 0

        lax.fori_loop(0, sz.full, w_sent, 0)
        for k in range(1, n):
            remote(k, sz.full, row_rem, sz.solid).wait_send()
            when_not_last(lax.rem(me + k, n), lambda: remote(k, sz.full + 1, row_odd, sz.short).wait_send())
        for q in (last - 2, last - 1):
            to_sib(q).wait_send()
            to_y(q).wait_send()
        for q in range(last - n_z, last - 1):
            to_z(q).wait_send()
        to_x(1).wait_send()
    with scope('t_send'):
        def sent(c, _):
            for cp in sends(c, chunk):
                cp.wait_send()
            return 0
        lax.fori_loop(0, sz.full, sent, 0)
        for cp in sends(sz.full, sz.rem):
            cp.wait_send()
    for r in range(ROUNDS):
        with scope(f't_gather{r}'):
            keep(r).wait()
            for cp in gathers(r):
                cp.wait_send()
            for jj in range(n_z - 1):
                onward(r, jj).wait_send()
            for zo in range(n_z):
                rcopy(gh.at[r], home(zo * 2 + 1 - at.y, r), ag_s.at[r, 0], fw_r.at[r, zo], y_peer).wait_recv()
    with scope('t_dw'):
        for k in range(1, n):
            src = lax.rem(me + n - k, n)
            rcopy(dw_hbm.at[pl.ds(0, sz.rows), :], dw_hbm.at[rows_at(src * sz.rows, sz.rows), :], dw_send.at[0, 0], dw_recv.at[k], sibling).wait_recv()


HBM = pl.BlockSpec(memory_space=pl.ANY)
VM = pl.BlockSpec(memory_space=pltpu.VMEM)
DMA = pltpu.SemaphoreType.DMA


def solution(mesh, chunk=CHUNK, tok=TOK, early=EARLY):
    n_fsdp, n_tp = mesh.shape['fsdp'], mesh.shape['tp']
    n_all, n_z = n_fsdp * n_tp, n_tp // 2
    S, V = jax.ShapeDtypeStruct, pltpu.VMEM
    i32 = jnp.int32

    def per_device(hidden, labels, tok_mask, norm_gain, w_rows):
        per_f, d = hidden.shape
        width, vocab_tp = w_rows.shape
        tokens, own = per_f * n_fsdp, per_f // n_tp
        half = own // ROUNDS
        sz = Sizes(vocab_tp, n_fsdp, chunk)
        n_low = sz.full - early[0] + 1

        dw_t, grad_hidden, sums, *_ = pl.pallas_call(
            functools.partial(head_kernel, sz, n_tp, vocab_tp, chunk, tok, early),
            out_shape=(S((n_fsdp * sz.rows, width), bf16), S(hidden.shape, bf16), S((1, d + 128), f32),
                       S((sz.rows, tokens), f32), S((sz.rows, tokens), bf16), S((tokens, d), bf16), S(((sz.full + 1) * chunk, d), bf16)),
            in_specs=[HBM, VM, VM, VM, HBM], out_specs=(HBM, HBM, VM, HBM, HBM, HBM, HBM),
            scratch_shapes=[
                V((tokens, d), bf16), V((sz.rows, d), bf16), *[V((chunk, tok), f32)] * 4, *[V((chunk, tok), bf16)] * 4, *[V((sz.rows, 2 * half), bf16)] * 2,
                V((8, tokens), f32), V((8, tokens), f32), V((1, tokens), f32), V((1, tokens), i32), V((n_fsdp, 1, per_f), i32), V((n_fsdp, 1, per_f), f32),
                V((2, tokens), f32), V((n_all, 2, own), f32), V((1, own), f32), V((1, tokens), f32), V((1, tokens), f32), V((8, min(128, half)), f32), V((own, d), bf16),
                V((chunk, d), f32), V((2, chunk, d), bf16), V((2, 2 * half, d), bf16), V((2, 2 * half, d), bf16), V((half, d), f32),
                V((2, half, d), bf16), V((6, half, d), bf16), V((3, half, d), f32), V((n_z - 1, half, d), bf16), V((ROUNDS, 2, n_z - 1, half, d), bf16), V((2, half, d), f32),
                V((half, d), bf16), V((ROUNDS, half, d), bf16), V((ROUNDS, half, d), bf16), V((1, d + 128), f32), V((n_all, 1, d + 128), f32),
                DMA((sz.full + 2, n_fsdp)), DMA((sz.full + 2, n_fsdp)), DMA((sz.full + 2,)), DMA((per_f // min(256, own),)), DMA((4,)), DMA((4,)), DMA((2, 2)), DMA((2, 2 * n_low)), DMA((2, 2)),
                DMA((n_all,)), DMA((n_all,)), DMA((n_all,)), DMA((n_all,)), DMA((2, n_fsdp)), DMA((2, n_fsdp)), DMA((2,)), DMA((2,)), DMA((2,)),
                DMA((n_z - 1, 2)), DMA((n_z - 1, 2)), DMA((n_z,)), DMA((n_z,)), DMA((n_tp,)), DMA((n_tp,)),
                DMA((1,)), DMA((2,)), DMA((sz.full + 1, 3)), DMA((n_fsdp,)), DMA((2,)), DMA((2,)), DMA((2,)), DMA((2,)), DMA((8,)),
                DMA((n_z - 1,)), DMA((ROUNDS, 2, n_z - 1)), DMA((1,)), DMA((ROUNDS,)),
                DMA((ROUNDS, n_z)), DMA((ROUNDS, n_z)), DMA((ROUNDS, n_z)), DMA((ROUNDS, n_z)), DMA((ROUNDS,)), DMA((n_all,)), DMA((n_all,))],
            compiler_params=pltpu.CompilerParams(vmem_limit_bytes=VMEM_LIMIT, collective_id=0, has_side_effects=True), name='head',
        )(hidden, labels[None, :], tok_mask[None, :], norm_gain, w_rows.T)
        return sums[0, d], grad_hidden, dw_t[:vocab_tp].T, sums[0, :d]

    return jax.shard_map(per_device, mesh=mesh, in_specs=(P('fsdp', None), P('fsdp'), P('fsdp'), P(), P('fsdp', 'tp')), out_specs=(P(), P('fsdp', None), P('fsdp', 'tp'), P()), check_vma=False)
```

profile of v0, /device:TPU:0, one launch (start us, length us, event | category | flops | bytes accessed | tf_op | source)
XLA Modules:
  0.0 417.1 jit_solution(5384455562685649337)
XLA Ops:
  0.6 402.6 %head.1 = (bf16[19008,256]{1,0:T(8,128)(2,1)}, bf16[2048,1024]{1,0:T(8,128)(2,1)}, f32[1,1152]{1,0:T(1,128)}, f32[4752,8192]{1,0:T(8,128)}, bf16[4752,8192]{1,0:...) custom-call(bf16[2048,1024]{1,0:T(8,128)(2,1)} %h_hbm.1, s32[1,2048]{1,0:T(1,128)} %bitcast.8, ...), custom_call_target="tpu_custom_call" | custom-call | tf_op jit(solution)/shard_map/head/pallas_call | solution.py:959
  403.3 1.1 slice.9
  404.4 0.0 copy-start
  404.4 1.4 slice.11
  405.8 9.3 %slice_bitcast_fusion = bf16[256,18992]{0,1:T(8,128)(2,1)} fusion(bf16[19008,256]{1,0:T(8,128)(2,1)} %get-tuple-element.9), kind=kLoop, calls=%fused_computation | loop fusion | bytes 19447808 | tf_op jit(solution)/shard_map/transpose | solution.py:979
  415.1 0.0 copy-done
  415.1 2.0 copy.10
Async XLA Ops:
  404.4 10.7 %copy-start = (bf16[2048,1024]{1,0:T(8,128)(2,1)S(1)}, bf16[2048,1024]{1,0:T(8,128)(2,1)}, u32[]{:S(2)}) copy-start(bf16[2048,1024]{1,0:T(8,128)(2,1)} %get-tuple-element.15) | copy-start | bytes 12582916
where the time goes:
time: 417 us
  Pallas kernels  403 us (97%)
  local copies, waits for them, and re-layouts  13.8 us (3%)
    pallas_call x1, Pallas kernels, per_device(): pl.pallas_call(functools.partial(head_kernel, sz, n_tp, vocab_tp, chunk,...  403 us
    transpose x1, local copies, waits for them, and re-layouts, per_device(): return (sums[0, d], grad_hidden, dw_t[:vocab_tp].T, sums[0, :d])  9.29 us

commit v1 on v0

--- a/solution.py
+++ b/solution.py
@@ -12,7 +12,7 @@
 NEG = -1e30
 CHUNK = 512
 TOK = 1024
-EARLY = (2, 5)
+EARLY = (3, 5)
 AHEAD = 5
 ROUNDS = 2
 VMEM_LIMIT = 67_043_328

time: 417 us -> 415 us (level)
  no operation moved by 1% of the time
where the time goes in v1:
time: 415 us
  Pallas kernels  401 us (97%)
  local copies, waits for them, and re-layouts  13.8 us (3%)
    pallas_call x1, Pallas kernels, per_device(): pl.pallas_call(functools.partial(head_kernel, sz, n_tp, vocab_tp, chunk,...  401 us
    transpose x1, local copies, waits for them, and re-layouts, per_device(): return (sums[0, d], grad_hidden, dw_t[:vocab_tp].T, sums[0, :d])  9.29 us

profile of v1, /device:TPU:0, one launch (start us, length us, event | category | flops | bytes accessed | tf_op | source)
XLA Modules:
  0.0 415.1 jit_solution(11914951047487612403)
XLA Ops:
  0.6 400.6 %head.1 = (bf16[19008,256]{1,0:T(8,128)(2,1)}, bf16[2048,1024]{1,0:T(8,128)(2,1)}, f32[1,1152]{1,0:T(1,128)}, f32[4752,8192]{1,0:T(8,128)}, bf16[4752,8192]{1,0:...) custom-call(bf16[2048,1024]{1,0:T(8,128)(2,1)} %h_hbm.1, s32[1,2048]{1,0:T(1,128)} %bitcast.8, ...), custom_call_target="tpu_custom_call" | custom-call | tf_op jit(solution)/shard_map/head/pallas_call | solution.py:959
  401.3 1.1 slice.9
  402.4 0.0 copy-start
  402.4 1.4 slice.11
  403.8 9.3 %slice_bitcast_fusion = bf16[256,18992]{0,1:T(8,128)(2,1)} fusion(bf16[19008,256]{1,0:T(8,128)(2,1)} %get-tuple-element.9), kind=kLoop, calls=%fused_computation | loop fusion | bytes 19447808 | tf_op jit(solution)/shard_map/transpose | solution.py:979
  413.1 0.0 copy-done
  413.1 2.0 copy.10
Async XLA Ops:
  402.4 10.7 %copy-start = (bf16[2048,1024]{1,0:T(8,128)(2,1)S(1)}, bf16[2048,1024]{1,0:T(8,128)(2,1)}, u32[]{:S(2)}) copy-start(bf16[2048,1024]{1,0:T(8,128)(2,1)} %get-tuple-element.15) | copy-start | bytes 12582916
